TPU v7x, 32 devices: a whole 2x2x4 slice. The times are simulated.
32 devices in a mesh: grp: 8 (over z, core), tp: 4 (over y, x).
Axes of the slice: x: 2, y: 2, z: 4, core: 2. Of those that a mesh axis runs over, the one named last changes fastest.
Arguments:
- tokens: bfloat16 [8192, 8192], P('grp'), may hold values from -12 to 12
- joined_weight: bfloat16 [8192, 10240], P(('grp', 'tp')), may hold values from -1.14904852 to 1.14904852
- rollout_lengths: int32 [64], P('grp'), may hold values from 1 to 128
- prompt_of: int32 [64, 1], P('grp'), may hold values from 0 to 7
- score_weight: bfloat16 [8192], P('tp'), may hold values from -0.52734375 to 0.52734375
Outputs:
- attention: bfloat16 [8192, 8192], P('grp', 'tp')
- advantages: float32 [64], P('grp')
All inputs are finite; a program needn't handle non-finite values.
Results may differ from a plain program's by a relative error of at most 0.012.
The roundings to bfloat16 on the way count: a program that leaves them out, or rounds other values in their place, can miss the bound.
Values may be sent and summed in bfloat16 or wider, within the bound.
A program may use at most 128 MiB of HBM per device.

v0:
```python
import jax
import jax.numpy as jnp
from jax import lax
from jax.sharding import PartitionSpec as P

QUERY_HEADS = 64
KV_HEAD_COUNT = 8
HEAD_SIZE = 128


def project_rows(block_rows, tokens):
    return jnp.dot(tokens, block_rows, preferred_element_type=jnp.float32)


def attend(joined_matrix, rollout_length_list):
    head_ratio = QUERY_HEADS // KV_HEAD_COUNT
    slot_index = joined_matrix.shape[0] // rollout_length_list.shape[0]
    groups = joined_matrix.shape[1] // ((head_ratio + 2) * HEAD_SIZE)
    reshaped_tensor = joined_matrix.reshape(
        rollout_length_list.shape[0], slot_index, groups, head_ratio + 2, HEAD_SIZE
    )
    queries = reshaped_tensor[:, :, :, :head_ratio, :]
    key_heads = reshaped_tensor[:, :, :, head_ratio, :]
    value_heads = reshaped_tensor[:, :, :, head_ratio + 1, :]
    scores = jnp.einsum(
        "rsgah,rtgh->rgast", queries, key_heads, preferred_element_type=jnp.float32
    ) * HEAD_SIZE ** (-0.5)
    positions = jnp.arange(slot_index)
    allowed = (positions[None, None, :] <= positions[None, :, None]) & (
        positions[None, None, :] < rollout_length_list[:, None, None]
    )
    scores = jnp.where(allowed[:, None, None], scores, jnp.float32(-1e30))
    peak = jnp.max(scores, axis=-1, keepdims=True)
    expo = jnp.exp(scores - peak)
    probs = (expo / jnp.sum(expo, axis=-1, keepdims=True)).astype(jnp.bfloat16)
    mixed = jnp.einsum("rgast,rtgh->rsgah", probs, value_heads, preferred_element_type=jnp.float32)
    return mixed.reshape(joined_matrix.shape[0], groups * head_ratio * HEAD_SIZE).astype(
        jnp.bfloat16
    )


def shards(tokens, joined_weight, rollout_lengths, prompt_of, score_weight):
    grp_count = lax.axis_size("grp")
    column_block = lax.all_to_all(joined_weight, "tp", split_axis=1, concat_axis=0, tiled=True)
    joined_matrix = project_rows(lax.all_gather(column_block, "grp", axis=0, tiled=True), tokens)
    attention = attend(joined_matrix.astype(jnp.bfloat16), rollout_lengths)
    partial_value = jnp.dot(attention, score_weight, preferred_element_type=jnp.float32)
    rollouts = rollout_lengths.shape[0]
    slot_index = tokens.shape[0] // rollouts
    valid = jnp.arange(slot_index)[None, :] < rollout_lengths[:, None]
    divisor_len = rollout_lengths.astype(jnp.float32)
    summed = lax.psum(partial_value, "tp")
    rewards = (
        jnp.sum(jnp.where(valid, summed.reshape(rollouts, slot_index), jnp.float32(0.0)), axis=1)
        / divisor_len
    )
    onehot = (prompt_of == jnp.arange(grp_count)[None, :]).astype(jnp.float32)
    counts, totals, squares = lax.psum(
        (
            jnp.sum(onehot, axis=0),
            jnp.sum(onehot * rewards[:, None], axis=0),
            jnp.sum(onehot * (rewards * rewards)[:, None], axis=0),
        ),
        "grp",
    )
    divisor = jnp.maximum(counts, 1.0)
    average = totals / divisor
    spread = squares / divisor - average * average
    own_mean = jnp.sum(onehot * average[None, :], axis=1)
    own_var = jnp.sum(onehot * spread[None, :], axis=1)
    advantages = (rewards - own_mean) / jnp.sqrt(own_var + 0.25)
    return (attention, advantages)


def solution(mesh):
    return jax.shard_map(
        shards,
        mesh=mesh,
        in_specs=(P("grp", None), P(("grp", "tp"), None), P("grp"), P("grp", None), P("tp")),
        out_specs=(P("grp", "tp"), P("grp")),
        check_vma=False,
    )
```

profile of v0, /device:TPU:0, one launch (start us, length us, event | category | flops | bytes accessed | tf_op | source)
XLA Modules:
  0.0 574.3 jit_solution(16208424381308565680)
XLA Ops:
  7.2 7.9 %copy.25 = bf16[256,10240]{0,1:T(8,128)(2,1)} copy(bf16[256,10240]{1,0:T(8,128)(2,1)} %param.6) | data formatting | bytes 10485760 | tf_op args[1]
  15.1 66.7 %all_to_all.19 = bf16[256,4,2560]{0,2,1:T(8,128)(2,1)} all-to-all(bf16[256,4,2560]{0,2,1:T(8,128)(2,1)} %bitcast.48), channel_id=1, replica_groups=mesh['grp'=8,'tp'=4] {'tp'}, dimensions={1} | all-to-all | bytes 10485760 | tf_op jit(solution)/shard_map/all_to_all | solution.py:44
  81.9 7.8 %copy.26 = bf16[4,256,2560]{2,1,0:T(8,128)(2,1)} copy(bf16[4,256,2560]{1,2,0:T(8,128)(2,1)} %bitcast.46) | data formatting | bytes 10485760 | tf_op jit(solution)/shard_map/all_to_all | solution.py:44
  89.8 0.1 iota_compare_fusion.2
  89.8 0.2 broadcast_and_fusion
  90.1 358.6 %all-gather.2.cloned.1.call-done = bf16[8192,2560]{1,0:T(8,128)(2,1)} async-done(((bf16[1024,2560]{1,0:T(8,128)(2,1)}), bf16[8192,2560]{1,0:T(8,128)(2,1)}) %all-gather.2.cloned.1.call-update) | async-done | bytes 41943056 | tf_op jit(solution)/shard_map/all_gather | solution.py:45
  448.6 53.3 %convolution_convert_fusion = bf16[1024,2560]{1,0:T(8,128)(2,1)} fusion(bf16[1024,8192]{1,0:T(8,128)(2,1)} %param.5, bf16[8192,2560]{1,0:T(8,128)(2,1)} %all-gather.2.cloned.1.call-done), kind=kOutput, calls=%fused_computation.5 | convolution fusion | flops 42952294400 | bytes 63963136 | tf_op jit(solution)/shard_map/dot_general | solution.py:12
  501.9 8.0 %copy.27 = bf16[1024,2560]{0,1:T(8,128)(2,1)} copy(bf16[1024,2560]{1,0:T(8,128)(2,1)} %convolution_convert_fusion) | data formatting | bytes 10485760 | tf_op jit(solution)/shard_map/convert_element_type | solution.py:46
  509.8 3.8 copy.39
  513.7 0.1 fusion.12
  513.8 2.3 slice.14
  516.1 0.4 copy.37
  516.4 3.5 fusion.2
  519.9 2.4 fusion.13
  522.3 3.3 convert_bitcast_fusion
  525.6 6.7 %copy.32 = bf16[8,128,2,8,128]{4,3,2,1,0:T(8,128)(2,1)} copy(bf16[8,128,2,8,128]{1,4,3,2,0:T(8,128)(2,1)} %convert_bitcast_fusion) | data formatting | bytes 8388608 | tf_op jit(solution)/shard_map/convert_element_type | solution.py:37
  532.3 7.3 %convert_element_type.25 = bf16[1024,2048]{1,0:T(8,128)(2,1)} reshape(bf16[8,128,2,8,128]{4,3,2,1,0:T(8,128)(2,1)} %copy.32) | data formatting | bytes 8388608 | tf_op jit(solution)/shard_map/convert_element_type | solution.py:37
  539.6 3.4 fusion.14
  543.0 9.8 %psum.28 = f32[8,128]{1,0:T(8,128)S(1)} all-reduce(f32[8,128]{1,0:T(8,128)S(1)} %bitcast.49), channel_id=1, replica_groups=mesh['grp'=8,'tp'=4] {'tp'}, use_global_device_ids=true, to_apply=%region_2.3 | all-reduce | flops 1024 | bytes 8192 | tf_op jit(solution)/shard_map/psum | solution.py:52
  552.8 0.2 select_reduce_fusion.4
  553.0 0.1 select_reduce_fusion.1
  553.1 13.6 %all-reduce = (f32[8]{0:T(128)S(1)}, f32[8]{0:T(128)S(1)}, f32[8]{0:T(128)S(1)}) all-reduce(f32[8]{0:T(128)S(1)} %get-tuple-element.6, f32[8]{0:T(128)S(1)} %get-tuple-element.5, f32[8]{0:T(128)S(1)} %get-tuple-element.4), channel_id=1, replica_groups=mesh['grp'=8,'tp'=4] {'grp'}, use_global_device_ids=true, to_apply=%region_5.6 | all-reduce | flops 24 | bytes 192 | tf_op jit(solution)/shard_map/psum | solution.py:58
  566.7 0.2 select_reduce_fusion.2
  566.9 0.5 rsqrt_multiply_fusion
  (12 shorter events, 0.1 us)
Async XLA Ops:
  7.2 441.4 %all-gather.2.cloned.1.call-start = ((), (), s32[]{:S(2)}) async-start(), calls=%async_computation.1 | async-start | bytes 47185920 | tf_op jit(solution)/shard_map/all_gather | solution.py:45
  81.9 7.8 %copy-start = (bf16[2048]{0:T(1024)(128)(2,1)S(1)}, bf16[2048]{0:T(1024)(128)(2,1)}, u32[]{:S(2)}) copy-start(bf16[2048]{0:T(1024)(128)(2,1)} %param.9) | copy-start | bytes 12292
  81.9 7.9 %copy-start.1 = (s32[8]{0:T(128)S(1)}, s32[8]{0:T(128)}, u32[]{:S(2)}) copy-start(s32[8]{0:T(128)} %param.7) | copy-start | bytes 100
  532.3 20.7 %copy-start.2 = (s32[8,1]{0,1:T(1,128)S(1)}, s32[8,1]{0,1:T(1,128)}, u32[]{:S(2)}) copy-start(s32[8,1]{0,1:T(1,128)} %param.8) | copy-start | bytes 100
Sparse Core Ops, SparseCore 0:
  89.8 358.7 all-gather.1
where the time goes:
time: 575 us; the launch traced here: 574 us
  waiting for transfers between devices  359 us (62%)
  blocking collectives  90.2 us (16%)
  matrix products  63.4 us (11%)
  local copies, waits for them, and re-layouts  44.3 us (8%)
  between operations  14.1 us (2%)
    all_gather x1, waiting for transfers between devices, shards(): lax.all_gather(column_block, 'grp', axis=0, tiled=True)  359 us
    all_to_all x1, blocking collectives, shards(): lax.all_to_all(joined_weight, 'tp', split_axis=1, concat_axis=0, tiled=True)  66.7 us
    dot_general x1, matrix products, project_rows(): return jnp.dot(tokens, block_rows, preferred_element_type=jnp.float32)  53.3 us
    convert_element_type x2, local copies, waits for them, and re-layouts, attend(): mixed.reshape(joined_matrix.shape[0], groups * head_ratio * HEAD_SIZE)  14 us
    psum x1, blocking collectives, shards(): lax.psum((jnp.sum(onehot, axis=0), jnp.sum(onehot * rewards[:, None], axi...  13.6 us
    unnamed x10, local copies, waits for them, and re-layouts  12.2 us
  transfers between devices with their start and end apart: 1, of which 1 were waited for; matrix products, arithmetic and copies ran while one was open for 0% of the time, Pallas kernels for 0%

commit v1 on v0

v1 whole, which is shorter than its diff:
```python
import functools

import jax
import jax.numpy as jnp
from jax import lax
from jax.experimental import pallas as pl
from jax.experimental.pallas import tpu as pltpu
from jax.sharding import PartitionSpec as P

QUERY_HEADS = 64
KV_HEAD_COUNT = 8
HEAD_SIZE = 128
CORES = 2
CHUNKS = 5


def attend_kernel(groups, chunks, lengths_ref, flag_ref, weight_ref, own, extra, out_ref, reward_ref):
    ratio = QUERY_HEADS // KV_HEAD_COUNT
    per_chunk = own.shape[2] // HEAD_SIZE
    slot = own.shape[1]
    length = lengths_ref[pl.program_id(0)]
    at_end = flag_ref[0] > 0

    def head(index):
        c, h = divmod(index, per_chunk)
        cols = slice(h * HEAD_SIZE, (h + 1) * HEAD_SIZE)
        added = jnp.where(at_end, extra[c, :, cols].astype(jnp.float32), jnp.float32(0.0))
        return (own[c, :, cols] + added).astype(jnp.bfloat16)

    s_pos = lax.broadcasted_iota(jnp.int32, (slot, slot), 0)
    t_pos = lax.broadcasted_iota(jnp.int32, (slot, slot), 1)
    allowed = ((t_pos <= s_pos) & (t_pos < length))[None]
    live = lax.broadcasted_iota(jnp.int32, (slot, HEAD_SIZE), 0) < length
    total = jnp.zeros((slot, HEAD_SIZE), jnp.float32)
    for g in range(groups):
        base = g * (ratio + 2)
        key = head(base + ratio)
        value = head(base + ratio + 1)
        queries = jnp.concatenate([head(base + a) for a in range(ratio)], axis=0)
        scores = lax.dot_general(
            queries, key, (((1,), (1,)), ((), ())), preferred_element_type=jnp.float32
        ) * HEAD_SIZE ** (-0.5)
        scores = jnp.where(allowed, scores.reshape(ratio, slot, slot), jnp.float32(-1e30))
        expo = jnp.exp(scores - jnp.max(scores, axis=-1, keepdims=True))
        probs = expo * (1.0 / jnp.sum(expo, axis=-1, keepdims=True))
        probs = probs.astype(jnp.bfloat16).reshape(ratio * slot, slot)
        mixed = jnp.dot(probs, value, preferred_element_type=jnp.float32).astype(jnp.bfloat16)
        for a in range(ratio):
            part = mixed[a * slot : (a + 1) * slot]
            cols = slice((g * ratio + a) * HEAD_SIZE, (g * ratio + a + 1) * HEAD_SIZE)
            out_ref[:, cols] = part
            total += part.astype(jnp.float32) * weight_ref[:, cols].astype(jnp.float32)
    summed = jnp.sum(jnp.where(live, total, jnp.float32(0.0)), axis=0, keepdims=True)
    summed = jnp.sum(summed, axis=1, keepdims=True)
    reward_ref[...] = jnp.broadcast_to(summed[None], reward_ref.shape)


def attend(own, extra, lengths, flag, score_weight):
    chunks, rows, width = own.shape
    rollouts = lengths.shape[0]
    slot = rows // rollouts
    features = score_weight.shape[0]
    ratio = QUERY_HEADS // KV_HEAD_COUNT
    block = pl.BlockSpec((chunks, slot, width), lambda r, *_: (0, r, 0))
    attention, reward = pl.pallas_call(
        functools.partial(attend_kernel, features // (ratio * HEAD_SIZE), chunks),
        grid_spec=pltpu.PrefetchScalarGridSpec(
            num_scalar_prefetch=2,
            grid=(rollouts,),
            in_specs=[pl.BlockSpec((1, features), lambda r, *_: (0, 0)), block, block],
            out_specs=[
                pl.BlockSpec((slot, features), lambda r, *_: (r, 0)),
                pl.BlockSpec((1, 8, HEAD_SIZE), lambda r, *_: (r, 0, 0)),
            ],
        ),
        out_shape=[
            jax.ShapeDtypeStruct((rows, features), jnp.bfloat16),
            jax.ShapeDtypeStruct((rollouts, 8, HEAD_SIZE), jnp.float32),
        ],
    )(lengths, flag, score_weight.reshape(1, features), own, extra)
    return attention, reward[:, 0, 0]


def project_kernel(
    n, tp_count, tokens, weight, own_out, extra, gath, far, prod,
    tok_v, far_v, w_v, acc, pbuf, send, recv, loads, w_sem, misc,
):
    g = lax.axis_index("grp")
    t = lax.axis_index("tp")
    z, core = g // CORES, g % CORES
    rows, depth = tokens.shape
    chunks, _, width = gath.shape
    own_rows = weight.shape[0]
    half = own_rows * tp_count
    plane = half * CORES
    columns = width * chunks
    part = rows // tp_count
    far_cols = far.shape[1]
    steps = n - 2
    inner = (z >= 1) & (z <= n - 2)
    helper = (z == 1) | (z == n - 2)
    at_end = (z == 0) | (z == n - 1)
    first_far = jnp.where(z < n // 2, 2, 0)
    ids = {}

    def sem(key):
        return ids.setdefault(key, len(ids))

    def remote(key, src, dst, device):
        i = sem(key)
        return pltpu.make_async_remote_copy(
            src_ref=src, dst_ref=dst, send_sem=send.at[i], recv_sem=recv.at[i],
            device_id=device, device_id_type=pl.DeviceIdType.MESH,
        )

    sends = []

    def start(cond, key, src, dst, device):
        @pl.when(cond)
        def _():
            remote(key, src, dst, device).start()

        sends.append((cond, key, src, dst, device))

    def arrived(cond, key, dst):
        @pl.when(cond)
        def _():
            remote(key, dst, dst, (g, t)).wait_recv()

    always = z >= 0
    sibling = (g + 1 - 2 * core, t)

    def piece(q, who):
        return gath.at[q, pl.ds(pl.multiple_of(z * plane + core * half + who * own_rows, own_rows), own_rows)]

    def block(q, p, c):
        return gath.at[q, pl.ds(pl.multiple_of(p * plane + c * half, half), half)]

    def columns_of(who, q):
        return weight.at[:, pl.ds(pl.multiple_of(who * columns + q * width, width), width)]

    def scatter(q):
        pltpu.make_async_copy(columns_of(t, q), piece(q, t), loads.at[q]).start()
        for d in range(1, tp_count):
            start(always, ("a", q, d), columns_of(t ^ d, q), piece(q, t), (g, t ^ d))

    def gathered(q):
        pltpu.make_async_copy(columns_of(t, q), piece(q, t), loads.at[q]).wait()
        for d in range(1, tp_count):
            arrived(always, ("a", q, d), piece(q, t ^ d))

    def launch(q):
        mine = block(q, z, core)
        start(z >= 1, ("l", q, 1), mine, mine, (g - CORES, t))
        start(z <= n - 2, ("r", q, 1), mine, mine, (g + CORES, t))
        start(always, ("s", q), mine, mine, sibling)

    def has(side, s):
        reach = (z + s <= n - 1) if side == "l" else (z - s >= 0)
        return reach if s == 1 else reach & inner

    def forward(q, s):
        for side, sign in (("l", 1), ("r", -1)):
            here = jnp.clip(z + sign * s, 0, n - 1)
            got = block(q, here, core)
            arrived(has(side, s), (side, q, s), got)
            if s < steps:
                more = (z >= 2) if side == "l" else (z <= n - 3)
                start(has(side, s) & more, (side, q, s + 1), got, got, (g - sign * CORES, t))
            start(has(side, s), ("s" + side, q, s), got, got, sibling)

    def swapped(q):
        arrived(always, ("s", q), block(q, z, 1 - core))
        for s in range(1, steps + 1):
            for side, sign in (("l", 1), ("r", -1)):
                here = jnp.clip(z + sign * s, 0, n - 1)
                arrived(has(side, s), ("s" + side, q, s), block(q, here, 1 - core))

    tile = 256

    def gemm(q, lhs, low, high, origin):
        def load(p):
            return pltpu.make_async_copy(
                gath.at[q, pl.ds(pl.multiple_of(p * plane, plane), plane)], w_v.at[p % 2], w_sem.at[p % 2]
            )

        load(low).start()
        acc[...] = jnp.zeros_like(acc)

        def step(p, carry):
            @pl.when(p + 1 < high)
            def _():
                load(p + 1).start()

            load(p).wait()
            cols = pl.ds(pl.multiple_of((p - origin) * plane, plane), plane)

            def rows_step(m, carry):
                at = pl.ds(pl.multiple_of(m * tile, tile), tile)
                acc[at, :] += jnp.dot(lhs[at, cols], w_v[p % 2], preferred_element_type=jnp.float32)
                return carry

            return lax.fori_loop(0, rows // tile, rows_step, carry)

        lax.fori_loop(low, high, step, 0)

    def compute(q):
        low = jnp.where(z == n - 1, n - 2, 0)
        high = jnp.where(z == 0, 2, n)
        gemm(q, tok_v, low, high, 0)
        out = pltpu.make_async_copy(acc, own_out.at[q], misc.at[1])
        out.start()
        out.wait()

    def assist(q):
        @pl.when(helper)
        def _():
            gemm(q, far_v, first_far, first_far + steps, first_far)
            pbuf[...] = acc[...].astype(pbuf.dtype)
            out = pltpu.make_async_copy(pbuf, prod.at[q], misc.at[2])
            out.start()
            out.wait()

        start(helper, ("p", q), prod.at[q], extra.at[q], (jnp.where(z == 1, g - CORES, g + CORES), t))

    def token_rows(who):
        return far.at[pl.ds(pl.multiple_of(who * part, part), part)]

    load_tokens = pltpu.make_async_copy(tokens, tok_v, misc.at[0])
    scatter(0)
    scatter(1)
    load_tokens.start()
    gathered(0)
    launch(0)
    far_source = tokens.at[
        pl.ds(pl.multiple_of(t * part, part), part),
        pl.ds(pl.multiple_of(first_far * plane, plane), far_cols),
    ]
    start(at_end, ("t",), far_source, token_rows(t), (jnp.where(z == 0, g + CORES, g - CORES), t))
    gathered(1)
    launch(1)
    load_tokens.wait()
    late = chunks - 2
    for q in range(chunks):
        if q + 2 < chunks:
            scatter(q + 2)
        if q == 1:
            arrived(helper, ("t",), token_rows(t))
            for d in range(1, tp_count):
                start(helper, ("g", d), token_rows(t), token_rows(t), (g, t ^ d))
        forward(q, 1)
        if q + 2 < chunks:
            gathered(q + 2)
            launch(q + 2)
        if q >= 1:
            for s in range(2, steps + 1):
                forward(q - 1, s)
            swapped(q - 1)
            compute(q - 1)
        if q == late:
            for d in range(1, tp_count):
                arrived(helper, ("g", d), token_rows(t ^ d))

            @pl.when(helper)
            def _():
                fill = pltpu.make_async_copy(far, far_v, misc.at[0])
                fill.start()
                fill.wait()

            for early in range(q - 1):
                assist(early)
        if q >= late and q >= 1:
            assist(q - 1)
    last = chunks - 1
    for s in range(2, steps + 1):
        forward(last, s)
    swapped(last)
    assist(last)
    compute(last)
    for q in range(chunks):
        arrived(at_end, ("p", q), extra.at[q])
    for cond, key, src, dst, device in sends:
        @pl.when(cond)
        def _():
            remote(key, src, dst, device).wait_send()


def project(tokens, weight, n, tp_count):
    rows, depth = tokens.shape
    own_rows = weight.shape[0]
    width = weight.shape[1] // tp_count // CHUNKS
    plane = own_rows * tp_count * CORES
    far = plane * (n - 2)
    flows = CHUNKS * (tp_count + 1 + 4 * (n - 2)) + tp_count
    anywhere = pl.BlockSpec(memory_space=pl.ANY)
    own, extra, *_ = pl.pallas_call(
        functools.partial(project_kernel, n, tp_count),
        in_specs=[anywhere] * 2,
        out_specs=[anywhere] * 5,
        out_shape=[
            jax.ShapeDtypeStruct((CHUNKS, rows, width), jnp.float32),
            jax.ShapeDtypeStruct((CHUNKS, rows, width), jnp.bfloat16),
            jax.ShapeDtypeStruct((CHUNKS, depth, width), jnp.bfloat16),
            jax.ShapeDtypeStruct((rows, far), jnp.bfloat16),
            jax.ShapeDtypeStruct((CHUNKS, rows, width), jnp.bfloat16),
        ],
        scratch_shapes=[
            pltpu.VMEM((rows, depth), jnp.bfloat16),
            pltpu.VMEM((rows, far), jnp.bfloat16),
            pltpu.VMEM((2, plane, width), jnp.bfloat16),
            pltpu.VMEM((rows, width), jnp.float32),
            pltpu.VMEM((rows, width), jnp.bfloat16),
            pltpu.SemaphoreType.DMA((flows,)),
            pltpu.SemaphoreType.DMA((flows,)),
            pltpu.SemaphoreType.DMA((CHUNKS,)),
            pltpu.SemaphoreType.DMA((2,)),
            pltpu.SemaphoreType.DMA((3,)),
        ],
        compiler_params=pltpu.CompilerParams(has_side_effects=True, vmem_limit_bytes=60 * 1024 * 1024),
    )(tokens, weight)
    return own, extra


def shards(tokens, joined_weight, rollout_lengths, prompt_of, score_weight):
    grp_count = lax.axis_size("grp")
    tp_count = lax.axis_size("tp")
    n = grp_count // CORES
    g = lax.axis_index("grp")
    z = g // CORES
    own, extra = project(tokens, joined_weight, n, tp_count)
    flag = ((z == 0) | (z == n - 1)).astype(jnp.int32).reshape(1)
    attention, reward = attend(own, extra, rollout_lengths, flag, score_weight)
    reward = reward / rollout_lengths.astype(jnp.float32)
    sent = jnp.stack([reward, prompt_of[:, 0].astype(jnp.float32)])
    gathered = lax.all_gather(sent, ("grp", "tp"), axis=0)
    gathered = gathered.reshape(grp_count, tp_count, 2, -1)
    everyone = jnp.sum(gathered[:, :, 0], axis=1).reshape(-1)
    prompts = gathered[:, 0, 1].reshape(-1, 1).astype(jnp.int32)
    labels = jnp.arange(grp_count)[None, :]
    onehot = (prompts == labels).astype(jnp.float32)
    counts = jnp.sum(onehot, axis=0)
    totals = jnp.sum(onehot * everyone[:, None], axis=0)
    squares = jnp.sum(onehot * (everyone * everyone)[:, None], axis=0)
    divisor = jnp.maximum(counts, 1.0)
    average = totals / divisor
    spread = squares / divisor - average * average
    mine = (prompt_of == labels).astype(jnp.float32)
    own_mean = jnp.sum(mine * average[None, :], axis=1)
    own_var = jnp.sum(mine * spread[None, :], axis=1)
    rewards = lax.dynamic_slice(everyone, (g * reward.shape[0],), reward.shape)
    advantages = (rewards - own_mean) / jnp.sqrt(own_var + 0.25)
    return (attention, advantages)


def solution(mesh):
    return jax.shard_map(
        shards,
        mesh=mesh,
        in_specs=(P("grp", None), P(("grp", "tp"), None), P("grp"), P("grp", None), P("tp")),
        out_specs=(P("grp", "tp"), P("grp")),
        check_vma=False,
    )
```

time: 575 us -> 438 us (0.76)
  Pallas kernels: 0 us -> 370 us
  waiting for transfers between devices: 359 us -> 0 us
  matrix products: 63.4 us -> 0 us
  local copies, waits for them, and re-layouts: 44.3 us -> 1.68 us
  blocking collectives: 90.2 us -> 64.7 us
  between operations: 14.1 us -> 0.74 us
    pallas_call x0 -> x2, Pallas kernels: none -> 370 us  [the longest x1 355 us: project(): pl.pallas_call(functools.partial(project_kernel, n, tp_count), in_specs=[...]
    all_gather x1 -> x0, waiting for transfers between devices: 359 us -> none  [shards(): lax.all_gather(column_block, 'grp', axis=0, tiled=True)]
    all_to_all x1 -> x0, blocking collectives: 66.7 us -> none  [shards(): lax.all_to_all(joined_weight, 'tp', split_axis=1, concat_axis=0, tiled=True)]
    all_gather x0 -> x1, blocking collectives: none -> 64.7 us  [shards(): gathered = lax.all_gather(sent, ('grp', 'tp'), axis=0)]
    dot_general x4 -> x0, matrix products: 63.4 us -> none  [the longest x1 53.3 us: project_rows(): return jnp.dot(tokens, block_rows, preferred_element_type=jnp.float32)]
    psum x2 -> x0, blocking collectives: 23.4 us -> none  [the longest x1 13.6 us: shards(): lax.psum((jnp.sum(onehot, axis=0), jnp.sum(onehot * rewards[:, None], axi...]
    convert_element_type x3 -> x1, local copies, waits for them, and re-layouts: 22 us -> 0.08 us  [shards(): prompts = gathered[:, 0, 1].reshape(-1, 1).astype(jnp.int32)]
    unnamed x10 -> x6, local copies, waits for them, and re-layouts: 12.2 us -> 0.02 us
  transfers between devices with their start and end apart: 1 -> 0, of which waited for: 1 -> 0; matrix products, arithmetic and copies ran while one was open for 0% -> 0% of each run, Pallas kernels for 0% -> 0%
where the time goes in v1:
time: 438 us
  Pallas kernels  370 us (84%)
  blocking collectives  64.7 us (15%)
    pallas_call x1, Pallas kernels, project(): pl.pallas_call(functools.partial(project_kernel, n, tp_count), in_specs=[...  355 us
    all_gather x1, blocking collectives, shards(): gathered = lax.all_gather(sent, ('grp', 'tp'), axis=0)  64.7 us
    pallas_call x1, Pallas kernels, attend(): pl.pallas_call(functools.partial(attend_kernel, features // (ratio * HEAD...  14.3 us

profile of v1, /device:TPU:0, one launch (start us, length us, event | category | flops | bytes accessed | tf_op | source)
XLA Modules:
  0.0 437.6 jit_solution(12167330137244585019)
XLA Ops:
  0.6 0.0 copy-start
  0.7 355.2 %shard_map.68 = (f32[5,1024,512]{2,1,0:T(8,128)}, bf16[5,1024,512]{2,1,0:T(8,128)(2,1)}, bf16[5,8192,512]{2,1,0:T(8,128)(2,1)}, bf16[1024,4096]{1,0:T(8,128)(2,1)}, bf16[5,1024,512]{2,1,0:T(8,128)(2,1)}) custom-call(bf16[1024,8192]{1,0:T(8,128)(2,1)} %tokens.1, bf16[256,10240]{1,0:T(8,128)(2,1)} %weight.1), custom_call_target="tpu_custom_call" | custom-call | tf_op jit(solution)/shard_map/pallas_call | solution.py:296
  355.9 0.0 copy-start.1
  355.9 0.0 copy-start.2
  355.9 0.0 copy-done
  355.9 0.6 reshape.60.weight_ref
  356.5 14.3 %shard_map.69 = (bf16[1024,2048]{1,0:T(8,128)(2,1)}, f32[8,8,128]{2,1,0:T(8,128)}) custom-call(s32[8]{0:T(128)} %lengths_ref.1, s32[1]{0:T(128)} %bitcast.flag_ref, bf16[1,2048]{1,0:T(2,128)(2,1)} %reshape.60.weight_ref, f32[5,1024,512]{2,1,0:T(8,128)} %get-tuple-element.6.own, bf16[5,1024,512]{2,1,0:T(8,128)(2,1)} %get-tuple-element.7.extra), custom_call_target="tpu_custom_call" | custom-call | tf_op jit(solution)/shard_map/pallas_call | solution.py:65
  370.8 0.9 slice_reduce_fusion.1
  371.7 0.0 copy-done.1
  371.7 0.0 copy-done.2
  371.8 64.7 %all-gather.1 = f32[32,2,8]{2,1,0:T(2,128)S(1)} all-gather(f32[1,2,8]{2,1,0:T(2,128)S(1)} %maximum_bitcast_fusion), channel_id=2, replica_groups=mesh['grp'=8,'tp'=4] {'grp','tp'}, dimensions={0}, use_global_device_ids=true | all-gather | bytes 2112 | tf_op jit(solution)/shard_map/all_gather | solution.py:335
  436.5 0.1 convert_element_type.36
  436.6 0.1 reshape.62
  436.7 0.1 select_reduce_fusion.1
  436.9 0.2 select_reduce_fusion.2
  437.0 0.6 rsqrt_multiply_fusion
  (8 shorter events, 0.1 us)
Async XLA Ops:
  0.6 355.3 %copy-start = (bf16[2048]{0:T(1024)(128)(2,1)S(1)}, bf16[2048]{0:T(1024)(128)(2,1)}, u32[]{:S(2)}) copy-start(bf16[2048]{0:T(1024)(128)(2,1)} %param.9) | copy-start | bytes 12292
  355.9 15.8 %copy-start.1 = (s32[8]{0:T(128)S(1)}, s32[8]{0:T(128)}, u32[]{:S(2)}) copy-start(s32[8]{0:T(128)} %lengths_ref.1) | copy-start | bytes 100
  355.9 15.8 %copy-start.2 = (s32[8,1]{0,1:T(1,128)S(1)}, s32[8,1]{0,1:T(1,128)}, u32[]{:S(2)}) copy-start(s32[8,1]{0,1:T(1,128)} %param.8) | copy-start | bytes 100

commit v2 on v1

--- a/solution.py
+++ b/solution.py
@@ -227,37 +227,28 @@
         return far.at[pl.ds(pl.multiple_of(who * part, part), part)]
 
     load_tokens = pltpu.make_async_copy(tokens, tok_v, misc.at[0])
-    scatter(0)
-    scatter(1)
-    load_tokens.start()
-    gathered(0)
-    launch(0)
     far_source = tokens.at[
         pl.ds(pl.multiple_of(t * part, part), part),
         pl.ds(pl.multiple_of(first_far * plane, plane), far_cols),
     ]
     start(at_end, ("t",), far_source, token_rows(t), (jnp.where(z == 0, g + CORES, g - CORES), t))
-    gathered(1)
-    launch(1)
+    for q in range(chunks):
+        scatter(q)
+    load_tokens.start()
+    for q in range(chunks):
+        gathered(q)
+        launch(q)
+    arrived(helper, ("t",), token_rows(t))
+    for d in range(1, tp_count):
+        start(helper, ("g", d), token_rows(t), token_rows(t), (g, t ^ d))
     load_tokens.wait()
-    late = chunks - 2
+    for q in range(chunks - 1):
+        forward(q, 1)
     for q in range(chunks):
-        if q + 2 < chunks:
-            scatter(q + 2)
-        if q == 1:
-            arrived(helper, ("t",), token_rows(t))
-            for d in range(1, tp_count):
-                start(helper, ("g", d), token_rows(t), token_rows(t), (g, t ^ d))
-        forward(q, 1)
-        if q + 2 < chunks:
-            gathered(q + 2)
-            launch(q + 2)
-        if q >= 1:
-            for s in range(2, steps + 1):
-                forward(q - 1, s)
-            swapped(q - 1)
-            compute(q - 1)
-        if q == late:
+        for s in range(2, steps + 1):
+            forward(q, s)
+        swapped(q)
+        if q == 0:
             for d in range(1, tp_count):
                 arrived(helper, ("g", d), token_rows(t ^ d))
 
@@ -267,16 +258,10 @@
                 fill.start()
                 fill.wait()
 
-            for early in range(q - 1):
-                assist(early)
-        if q >= late and q >= 1:
-            assist(q - 1)
-    last = chunks - 1
-    for s in range(2, steps + 1):
-        forward(last, s)
-    swapped(last)
-    assist(last)
-    compute(last)
+        assist(q)
+        if q == 0:
+            forward(chunks - 1, 1)
+        compute(q)
     for q in range(chunks):
         arrived(at_end, ("p", q), extra.at[q])
     for cond, key, src, dst, device in sends:
@@ -321,6 +306,56 @@
     return own, extra
 
 
+def share_kernel(grp_count, tp_count, mine, out, held, send, recv, local):
+    g = lax.axis_index("grp")
+    t = lax.axis_index("tp")
+
+    def copy(i, src, dst, device):
+        return pltpu.make_async_remote_copy(
+            src_ref=src, dst_ref=dst, send_sem=send.at[i], recv_sem=recv.at[i],
+            device_id=device, device_id_type=pl.DeviceIdType.MESH,
+        )
+
+    own = pltpu.make_async_copy(mine, held.at[g, t], local)
+    own.start()
+    first = [copy(d - 1, mine, held.at[g, t], (g, t ^ d)) for d in range(1, tp_count)]
+    for c in first:
+        c.start()
+    own.wait()
+    for d in range(1, tp_count):
+        copy(d - 1, mine, held.at[g, t ^ d], (g, t)).wait_recv()
+    second = [
+        copy(tp_count - 1 + d - 1, held.at[g], held.at[g], ((g + d) % grp_count, t))
+        for d in range(1, grp_count)
+    ]
+    for c in second:
+        c.start()
+    for d in range(1, grp_count):
+        source = held.at[(g + grp_count - d) % grp_count]
+        copy(tp_count - 1 + d - 1, source, source, (g, t)).wait_recv()
+    for c in first + second:
+        c.wait_send()
+    out[...] = held[...]
+
+
+def share(mine, grp_count, tp_count):
+    shape = (grp_count, tp_count) + mine.shape
+    flows = grp_count + tp_count - 2
+    return pl.pallas_call(
+        functools.partial(share_kernel, grp_count, tp_count),
+        in_specs=[pl.BlockSpec(memory_space=pl.ANY)],
+        out_specs=pl.BlockSpec(memory_space=pltpu.VMEM),
+        out_shape=jax.ShapeDtypeStruct(shape, mine.dtype),
+        scratch_shapes=[
+            pltpu.VMEM(shape, mine.dtype),
+            pltpu.SemaphoreType.DMA((flows,)),
+            pltpu.SemaphoreType.DMA((flows,)),
+            pltpu.SemaphoreType.DMA,
+        ],
+        compiler_params=pltpu.CompilerParams(has_side_effects=True),
+    )(mine)
+
+
 def shards(tokens, joined_weight, rollout_lengths, prompt_of, score_weight):
     grp_count = lax.axis_size("grp")
     tp_count = lax.axis_size("tp")
@@ -332,8 +367,9 @@
     attention, reward = attend(own, extra, rollout_lengths, flag, score_weight)
     reward = reward / rollout_lengths.astype(jnp.float32)
     sent = jnp.stack([reward, prompt_of[:, 0].astype(jnp.float32)])
-    gathered = lax.all_gather(sent, ("grp", "tp"), axis=0)
-    gathered = gathered.reshape(grp_count, tp_count, 2, -1)
+    count = reward.shape[0]
+    sent = jnp.pad(sent, ((0, -2 % 8), (0, -count % 128)))
+    gathered = share(sent, grp_count, tp_count)[:, :, :2, :count]
     everyone = jnp.sum(gathered[:, :, 0], axis=1).reshape(-1)
     prompts = gathered[:, 0, 1].reshape(-1, 1).astype(jnp.int32)
     labels = jnp.arange(grp_count)[None, :]

time: 438 us -> 334 us (0.76)
  blocking collectives: 64.7 us -> 0 us
  Pallas kernels: 370 us -> 328 us
    all_gather x1 -> x0, blocking collectives: 64.7 us -> none  [shards(): gathered = lax.all_gather(sent, ('grp', 'tp'), axis=0)]
    pallas_call x1, Pallas kernels: 355 us -> 299 us  [project(): pl.pallas_call(functools.partial(project_kernel, n, tp_count), in_specs=[...]
    pallas_call x0 -> x1, Pallas kernels: none -> 14.2 us  [share(): pl.pallas_call(functools.partial(share_kernel, grp_count, tp_count), in_s...]
where the time goes in v2:
time: 334 us; the launch traced here: 333 us
  Pallas kernels  328 us (98%)
    pallas_call x1, Pallas kernels, project(): pl.pallas_call(functools.partial(project_kernel, n, tp_count), in_specs=[...  299 us
    pallas_call x1, Pallas kernels, attend(): pl.pallas_call(functools.partial(attend_kernel, features // (ratio * HEAD...  14.3 us
    pallas_call x1, Pallas kernels, share(): pl.pallas_call(functools.partial(share_kernel, grp_count, tp_count), in_s...  14.2 us

profile of v2, /device:TPU:0, one launch (start us, length us, event | category | flops | bytes accessed | tf_op | source)
XLA Modules:
  0.0 333.4 jit_solution(12010889512538608317)
XLA Ops:
  0.6 0.0 copy-start
  0.7 299.3 %shard_map.68 = (f32[5,1024,512]{2,1,0:T(8,128)}, bf16[5,1024,512]{2,1,0:T(8,128)(2,1)}, bf16[5,8192,512]{2,1,0:T(8,128)(2,1)}, bf16[1024,4096]{1,0:T(8,128)(2,1)}, bf16[5,1024,512]{2,1,0:T(8,128)(2,1)}) custom-call(bf16[1024,8192]{1,0:T(8,128)(2,1)} %tokens.1, bf16[256,10240]{1,0:T(8,128)(2,1)} %weight.1), custom_call_target="tpu_custom_call" | custom-call | tf_op jit(solution)/shard_map/pallas_call | solution.py:281
  300.0 0.0 copy-start.1
  300.0 0.0 copy-start.2
  300.0 0.0 copy-done
  300.0 0.6 reshape.57.weight_ref
  300.6 14.3 %shard_map.69 = (bf16[1024,2048]{1,0:T(8,128)(2,1)}, f32[8,8,128]{2,1,0:T(8,128)}) custom-call(s32[8]{0:T(128)} %lengths_ref.1, s32[1]{0:T(128)} %bitcast.flag_ref, bf16[1,2048]{1,0:T(2,128)(2,1)} %reshape.57.weight_ref, f32[5,1024,512]{2,1,0:T(8,128)} %get-tuple-element.6.own, bf16[5,1024,512]{2,1,0:T(8,128)(2,1)} %get-tuple-element.7.extra), custom_call_target="tpu_custom_call" | custom-call | tf_op jit(solution)/shard_map/pallas_call | solution.py:65
  314.9 0.9 slice_reduce_fusion.1
  315.8 0.0 copy-done.1
  315.8 0.0 copy-done.2
  315.8 0.6 select_maximum_fusion.mine
  316.4 14.2 %shard_map.70 = f32[8,4,8,128]{3,2,1,0:T(8,128)} custom-call(f32[8,128]{1,0:T(8,128)} %select_maximum_fusion.mine), custom_call_target="tpu_custom_call" | custom-call | tf_op jit(solution)/shard_map/pallas_call | solution.py:344
  330.6 0.9 slice_reduce_fusion
  331.5 0.1 reshape.58
  331.6 0.8 convert_reduce_fusion.1
  332.4 0.1 convert_element_type.38
  332.4 0.1 select_reduce_fusion.1
  332.6 0.2 select_reduce_fusion.2
  332.8 0.6 rsqrt_multiply_fusion
  (4 shorter events, 0.0 us)
Async XLA Ops:
  0.6 299.3 %copy-start = (bf16[2048]{0:T(1024)(128)(2,1)S(1)}, bf16[2048]{0:T(1024)(128)(2,1)}, u32[]{:S(2)}) copy-start(bf16[2048]{0:T(1024)(128)(2,1)} %param.9) | copy-start | bytes 12292
  300.0 15.8 %copy-start.1 = (s32[8]{0:T(128)S(1)}, s32[8]{0:T(128)}, u32[]{:S(2)}) copy-start(s32[8]{0:T(128)} %lengths_ref.1) | copy-start | bytes 100
  300.0 15.8 %copy-start.2 = (s32[8,1]{0,1:T(1,128)S(1)}, s32[8,1]{0,1:T(1,128)}, u32[]{:S(2)}) copy-start(s32[8,1]{0,1:T(1,128)} %param.8) | copy-start | bytes 100
